TPU v7x, 32 devices: a whole 2x2x4 slice. The times are simulated.
32 devices in a mesh: dp: 8 (over z, y), section: 4 (over x, core).
Axes of the slice: x: 2, y: 2, z: 4, core: 2. Of those that a mesh axis runs over, the one named last changes fastest.
Arguments:
- real_in: bfloat16 [64, 144, 512], P('dp'), may hold values from -48 to 48
- fake_in: bfloat16 [64, 144, 512], P('dp'), may hold values from -48 to 48
- kernel_first: bfloat16 [5, 512, 1024], P(None, None, 'section'), may hold values from -0.15625 to 0.15625
- kernel_second: bfloat16 [5, 1024, 1024], P(None, None, 'section'), may hold values from -0.125 to 0.125
Outputs:
- layer_loss: float32 [2], replicated
- grad_first: float32 [512, 5, 1024], P('dp', None, 'section')
- grad_second: float32 [1024, 5, 1024], P('dp', None, 'section')
All inputs are finite; a program needn't handle non-finite values.
Results may differ from a plain program's by a relative error of at most 0.012.
The roundings to bfloat16 on the way count: a program that leaves them out, or rounds other values in their place, can miss the bound.
Values may be sent and summed in bfloat16 or wider, within the bound.
A program may use at most 128 MiB of HBM per device.

v0:
```python
import jax
import jax.numpy as jnp
from jax import lax
from jax.sharding import PartitionSpec as P

K = 5


smooth_width = 0.1
leak_slope = 0.1


def conv_strided(values, kernel, frames):
    padded = jnp.pad(values, ((0, 0), (2, 2), (0, 0)))
    summed = jnp.zeros((values.shape[0] * frames, kernel.shape[2]), jnp.float32)
    for tap in range(kernel.shape[0]):
        window = padded[:, tap : tap + 3 * frames - 2 : 3].reshape(-1, values.shape[2])
        summed = summed + jnp.dot(window, kernel[tap], preferred_element_type=jnp.float32)
    return summed.reshape(values.shape[0], frames, -1)


def conv_forward(values, kernel):
    frames = values.shape[1]
    padded = jnp.pad(values, ((0, 0), (2, 2), (0, 0)))
    summed = jnp.zeros((values.shape[0] * frames, kernel.shape[2]), jnp.float32)
    for tap in range(kernel.shape[0]):
        window = padded[:, tap : tap + frames].reshape(-1, values.shape[2])
        summed = summed + jnp.dot(window, kernel[tap], preferred_element_type=jnp.float32)
    return summed.reshape(values.shape[0], frames, -1)


def conv_backward(delta, kernel):
    frames = delta.shape[1]
    padded = jnp.pad(delta, ((0, 0), (2, 2), (0, 0)))
    summed = jnp.zeros((delta.shape[0] * frames, kernel.shape[1]), jnp.float32)
    for tap in range(kernel.shape[0]):
        window = padded[:, 4 - tap : 4 - tap + frames].reshape(-1, delta.shape[2])
        summed = summed + lax.dot_general(
            window, kernel[tap], (((1,), (1,)), ((), ())), preferred_element_type=jnp.float32
        )
    return summed.reshape(delta.shape[0], frames, -1)


def weight_term(values, delta, amount, stride):
    frames = delta.shape[1]
    padded = jnp.pad(values, ((0, 0), (2, 2), (0, 0)))
    flat_delta = delta.reshape(-1, delta.shape[2])
    pieces = []
    for tap in range(K):
        window = padded[:, tap : tap + stride * (frames - 1) + 1 : stride].reshape(-1, amount)
        pieces.append(
            lax.dot_general(
                window, flat_delta, (((0,), (0,)), ((), ())), preferred_element_type=jnp.float32
            )
        )
    return jnp.stack(pieces, axis=1)


def activate(pre):
    return jnp.where(pre > 0, pre, leak_slope * pre).astype(jnp.bfloat16)


def local_grad(feature, normaliser):
    half = feature.shape[0] // 2
    difference = feature[:half].astype(jnp.float32) - feature[half:].astype(jnp.float32)
    slope = (
        difference / jnp.sqrt(difference * difference + smooth_width * smooth_width) / normaliser
    )
    return jnp.concatenate([slope, -slope], axis=0)


def smooth_total(feature):
    half = feature.shape[0] // 2
    difference = feature[:half].astype(jnp.float32) - feature[half:].astype(jnp.float32)
    return jnp.sum(jnp.sqrt(difference * difference + smooth_width * smooth_width) - smooth_width)


def shards(real_in, fake_in, kernel_first, kernel_second):
    replicas = lax.axis_size("dp")
    frames = real_in.shape[1] // 3
    in_width = real_in.shape[2]
    width = kernel_second.shape[1]
    normaliser = float(real_in.shape[0] * frames)
    count_all = float(real_in.shape[0] * replicas * frames * width)
    values = jnp.concatenate([real_in, fake_in], axis=0)
    first = activate(conv_strided(values, kernel_first, frames))
    partial_first = smooth_total(first)
    total_first = lax.psum(partial_first, ("dp", "section"))
    whole_first = lax.all_gather(first, "section", axis=2, tiled=True)
    second = activate(conv_forward(whole_first, kernel_second))
    partial_second = smooth_total(second)
    total_second = lax.psum(partial_second, ("dp", "section"))
    layer_loss = jnp.stack([total_first, total_second]) / count_all
    delta_second = (local_grad(second, normaliser) * jnp.where(second > 0, 1.0, leak_slope)).astype(
        jnp.bfloat16
    )
    upstream_terms = conv_backward(delta_second, kernel_second)
    upstream = lax.psum_scatter(upstream_terms, "section", scatter_dimension=2, tiled=True).astype(
        jnp.bfloat16
    )
    delta_first = (
        (local_grad(first, normaliser) + upstream.astype(jnp.float32))
        * jnp.where(first > 0, 1.0, leak_slope)
    ).astype(jnp.bfloat16)
    term_first = weight_term(values, delta_first, in_width, 3)
    term_second = weight_term(whole_first, delta_second, width, 1)
    grad_first, grad_second = (
        lax.psum_scatter(term_first, "dp", scatter_dimension=0, tiled=True),
        lax.psum_scatter(term_second, "dp", scatter_dimension=0, tiled=True),
    )
    return (layer_loss, grad_first, grad_second)


def solution(mesh):
    return jax.shard_map(
        shards,
        mesh=mesh,
        in_specs=(
            P("dp", None, None),
            P("dp", None, None),
            P(None, None, "section"),
            P(None, None, "section"),
        ),
        out_specs=(P(), P("dp", None, "section"), P("dp", None, "section")),
        check_vma=False,
    )
```

profile of v0, /device:TPU:0, one launch (start us, length us, event | category | flops | bytes accessed | tf_op | source)
XLA Modules:
  0.0 297.8 jit_solution(13999572047257641910)
XLA Ops:
  7.2 2.6 fusion.3
  9.9 1.2 slice.102
  11.1 3.4 %slice.104 = bf16[16,48,512]{2,1,0:T(8,128)(2,1)} slice(bf16[16,148,512]{2,1,0:T(8,128)(2,1)S(1)} %fusion.3), slice={[0:16:1], [1:143:3], [0:512:1]} | slice | bytes 1572864 | tf_op jit(solution)/shard_map/slice | solution.py:17
  14.4 3.3 %slice.106 = bf16[16,48,512]{2,1,0:T(8,128)(2,1)} slice(bf16[16,148,512]{2,1,0:T(8,128)(2,1)S(1)} %fusion.3), slice={[0:16:1], [2:144:3], [0:512:1]} | slice | bytes 1572864 | tf_op jit(solution)/shard_map/slice | solution.py:17
  17.7 3.4 %slice.108 = bf16[16,48,512]{2,1,0:T(8,128)(2,1)} slice(bf16[16,148,512]{2,1,0:T(8,128)(2,1)S(1)} %fusion.3), slice={[0:16:1], [3:145:3], [0:512:1]} | slice | bytes 1572864 | tf_op jit(solution)/shard_map/slice | solution.py:17
  21.1 3.4 %slice.110 = bf16[16,48,512]{2,1,0:T(8,128)(2,1)} slice(bf16[16,148,512]{2,1,0:T(8,128)(2,1)S(1)} %fusion.3), slice={[0:16:1], [4:146:3], [0:512:1]} | slice | bytes 1572864 | tf_op jit(solution)/shard_map/slice | solution.py:17
  24.5 1.5 fusion.49
  25.9 1.6 convolution_add_fusion.7
  27.6 0.4 convolution_add_fusion.6
  28.0 0.4 convolution_add_fusion.5
  28.3 0.4 copy-done.6
  28.7 0.4 convolution_add_fusion.4
  29.1 0.9 fusion.14
  30.0 22.6 %all-gather.2.cloned.1.call-done = bf16[16,48,1024]{2,1,0:T(8,128)(2,1)} async-done(((bf16[16,48,256]{2,1,0:T(8,128)(2,1)}), bf16[16,48,1024]{2,1,0:T(8,128)(2,1)}) %all-gather.2.cloned.1.call-update) | async-done | bytes 1572880 | tf_op jit(solution)/shard_map/all_gather | solution.py:89
  52.7 6.3 %pad_slice_fusion = (bf16[16,48,1024]{2,1,0:T(8,128)(2,1)S(1)}, bf16[16,48,1024]{2,1,0:T(8,128)(2,1)S(1)}, bf16[16,48,1024]{2,1,0:T(8,128)(2,1)S(1)}, bf16[16,48,1024]{2,1,0:T(8,128)(2,1)S(1)}) fusion(bf16[16,48,1024]{2,1,0:T(8,128)(2,1)} %all-gather.2.cloned.1.call-done), kind=kLoop, calls=%fused_computation.10 | loop fusion | bytes 7864320 | tf_op jit(solution)/shard_map/slice | solution.py:27
  59.0 0.6 fusion.33
  59.6 0.6 convolution_add_fusion.3
  60.2 0.8 copy-done.1
  61.0 0.6 convolution_add_fusion.2
  61.6 0.6 convolution_add_fusion.1
  62.2 0.6 convolution_add_fusion
  62.9 0.8 fusion.56
  64.1 0.6 fusion.25
  64.7 0.5 pad_slice_fusion.4
  65.2 0.6 fusion.22
  65.8 0.6 fusion.28
  66.4 0.6 fusion.31
  67.0 2.5 add_add_fusion
  69.5 0.2 reduce-scatter.8.cloned.1.call-start
  69.7 1.1 copy-done.2
  71.0 1.6 fusion.8
  72.5 1.6 fusion.7
  74.2 1.6 fusion.6
  75.7 1.6 fusion.5
  77.4 1.6 fusion.4
  79.0 0.9 copy-done.3
  80.0 0.8 fusion.57
  80.8 26.6 %reduce-scatter.4.cloned.1.call-done = f32[16,48,256]{2,1,0:T(8,128)} async-done(((f32[16,48,1024]{2,1,0:T(8,128)}), f32[16,48,256]{2,1,0:T(8,128)}) %reduce-scatter.4.cloned.1.call-update) | async-done | bytes 786448 | tf_op jit(solution)/shard_map/reduce_scatter | solution.py:98
  107.4 1.4 fusion.18
  108.8 1.2 fusion.13
  110.0 1.2 fusion.12
  111.3 1.2 fusion.11
  112.5 1.2 fusion.10
  113.7 1.2 fusion.9
  114.9 42.5 %all-reduce.3 = (f32[1]{0:T(128)}, f32[1]{0:T(128)}) all-reduce(f32[1]{0:T(128)} %bitcast.23, f32[1]{0:T(128)} %bitcast.11), channel_id=1, replica_groups=mesh['dp'=8,'section'=4] {'dp','section'}, use_global_device_ids=true, to_apply=%region_3.4 | all-reduce | flops 2 | bytes 16 | tf_op jit(solution)/shard_map/psum | solution.py:92
  157.4 1.8 maximum_multiply_fusion
  159.2 56.9 %reduce-scatter.8.cloned.1.call-done = f32[128,5,256]{2,0,1:T(8,128)} async-done(((f32[1024,5,256]{2,0,1:T(8,128)}), f32[128,5,256]{2,0,1:T(8,128)}) %reduce-scatter.8.cloned.1.call-update) | async-done | bytes 655376 | tf_op jit(solution)/shard_map/reduce_scatter | solution.py:109
  216.1 75.2 %reduce-scatter.6.cloned.1.call-done = f32[64,5,256]{2,0,1:T(8,128)} async-done(((f32[512,5,256]{2,0,1:T(8,128)}), f32[64,5,256]{2,0,1:T(8,128)}) %reduce-scatter.6.cloned.1.call-update) | async-done | bytes 327696 | tf_op jit(solution)/shard_map/reduce_scatter | solution.py:108
  (38 shorter events, 0.8 us)
Async XLA Ops:
  7.2 45.5 %all-gather.2.cloned.1.call-start = ((), (), s32[]{:S(2)}) async-start(), calls=%async_computation.3 | async-start | bytes 1966080 | tf_op jit(solution)/shard_map/all_gather | solution.py:89
  11.1 13.4 %copy-start.4 = (bf16[16,48,512]{2,1,0:T(8,128)(2,1)}, bf16[16,48,512]{2,1,0:T(8,128)(2,1)S(1)}, u32[]{:S(2)}) copy-start(bf16[16,48,512]{2,1,0:T(8,128)(2,1)S(1)} %slice.102) | copy-start | bytes 2359300
  24.4 3.1 %copy-start.10 = (bf16[16,48,512]{2,1,0:T(8,128)(2,1)S(1)}, bf16[16,48,512]{2,1,0:T(8,128)(2,1)}, u32[]{:S(2)}) copy-start(bf16[16,48,512]{2,1,0:T(8,128)(2,1)} %slice.106) | copy-start | bytes 2359300
  24.4 3.1 %copy-start.15 = (bf16[5,512,256]{2,1,0:T(8,128)(2,1)S(1)}, bf16[5,512,256]{2,1,0:T(8,128)(2,1)}, u32[]{:S(2)}) copy-start(bf16[5,512,256]{2,1,0:T(8,128)(2,1)} %param.6) | copy-start | bytes 3932164
  25.9 2.0 copy-start.8
  27.6 1.1 copy-start.6
  30.0 29.0 %copy-start = (bf16[5,1024,256]{2,1,0:T(8,128)(2,1)S(1)}, bf16[5,1024,256]{2,1,0:T(8,128)(2,1)}, u32[]{:S(2)}) copy-start(bf16[5,1024,256]{2,1,0:T(8,128)(2,1)} %param.7) | copy-start | bytes 7864324
  30.0 77.4 %reduce-scatter.4.cloned.1.call-start = ((), (), s32[]{:S(2)}) async-start(), calls=%async_computation.4 | async-start | bytes 3932160 | tf_op jit(solution)/shard_map/reduce_scatter | solution.py:98
  59.6 1.4 copy-start.1
  63.9 0.8 copy-start.13
  69.5 1.4 copy-start.2
  69.5 1.5 copy-start.14
  69.5 146.6 %reduce-scatter.8.cloned.1.call-start = ((), (), s32[]{:S(2)}) async-start(), calls=%async_computation.6 | async-start | bytes 5898240 | tf_op jit(solution)/shard_map/reduce_scatter | solution.py:109
  79.0 1.0 copy-start.3
  79.0 29.8 %copy-start.5 = (bf16[16,48,512]{2,1,0:T(8,128)(2,1)S(1)}, bf16[16,48,512]{2,1,0:T(8,128)(2,1)}, u32[]{:S(2)}) copy-start(bf16[16,48,512]{2,1,0:T(8,128)(2,1)} %copy-done.4) | copy-start | bytes 2359300
  79.0 212.2 %reduce-scatter.6.cloned.1.call-start = ((), (), s32[]{:S(2)}) async-start(), calls=%async_computation.5 | async-start | bytes 2949120 | tf_op jit(solution)/shard_map/reduce_scatter | solution.py:108
  108.8 1.3 copy-start.12
  110.0 1.2 copy-start.11
  111.3 1.2 copy-start.9
  112.5 1.2 copy-start.7
Sparse Core Ops, SparseCore 0:
  30.1 22.5 all-gather.1
  69.6 37.7 reduce-scatter.3
  111.6 104.4 reduce-scatter.7
  220.0 71.1 reduce-scatter.5
where the time goes:
time: 298 us
  waiting for transfers between devices  181 us (61%)
  blocking collectives  42.5 us (14%)
  matrix products  26.1 us (9%)
  local copies, waits for them, and re-layouts  24.7 us (8%)
  between operations  14 us (5%)
  other arithmetic  8.82 us (3%)
    reduce_scatter x1, waiting for transfers between devices, shards(): lax.psum_scatter(term_first, 'dp', scatter_dimension=0, tiled=True)  75.2 us
    reduce_scatter x1, waiting for transfers between devices, shards(): lax.psum_scatter(term_second, 'dp', scatter_dimension=0, tiled=True)  56.9 us
    psum x1, blocking collectives, shards(): total_second = lax.psum(partial_second, ('dp', 'section'))  42.5 us
    reduce_scatter x1, waiting for transfers between devices, shards(): lax.psum_scatter(upstream_terms, 'section', scatter_dimension=2, tiled=True)  26.6 us
    all_gather x1, waiting for transfers between devices, shards(): whole_first = lax.all_gather(first, 'section', axis=2, tiled=True)  22.6 us
    slice x5, local copies, waits for them, and re-layouts, conv_strided(): window = padded[:, tap:tap + 3 * frames - 2:3].reshape(-1, values.shape[2])  14.6 us
    dot_general x10, matrix products, weight_term(): lax.dot_general(window, flat_delta, (((0,), (0,)), ((), ())), preferred_e...  14.1 us
    slice x1, local copies, waits for them, and re-layouts, conv_forward(): window = padded[:, tap:tap + frames].reshape(-1, values.shape[2])  6.32 us
  transfers between devices with their start and end apart: 4, of which 4 were waited for; matrix products, arithmetic and copies ran while one was open for 6% of the time, Pallas kernels for 0%

commit v1 on v0

v1 whole, which is shorter than its diff:
```python
import functools

import jax
import jax.numpy as jnp
from jax import lax
from jax.experimental import pallas as pl
from jax.experimental.pallas import tpu as pltpu
from jax.sharding import PartitionSpec as P

smooth_width = 0.1
leak_slope = 0.1
F32 = jnp.float32
BF16 = jnp.bfloat16
MESH = pl.DeviceIdType.MESH


def dot(a, b, ca=1, cb=0):
    return lax.dot_general(a, b, (((ca,), (cb,)), ((), ())), preferred_element_type=F32)


def leaky(pre):
    return jnp.where(pre > 0, pre, leak_slope * pre).astype(BF16)


def kernel(
    ndp, nsec, frames, normaliser,
    real, fake, w1h, w2h,
    loss_o, g1_o, g2_o,
    x, w1, w2, hall, acc, slopes, dk, us, ur, own_up, s2, s1, r2, r1, lsec, ldp,
    in_sem, hs, hr, uss, urs, g2s, g2r, g1s, g1r, lss, lsr, lds, ldr,
):
    dp, sec = lax.axis_index("dp"), lax.axis_index("section")
    rows, width = acc.shape
    half = rows // 2
    taps = w2.shape[0]
    cin = g1_o.shape[1] * ndp
    c2, c1 = g2_o.shape[1], g1_o.shape[1]

    def sec_at(j):
        return lax.rem(sec + j, nsec)

    def dp_at(j):
        return lax.rem(dp + j, ndp)

    loads = [
        pltpu.make_async_copy(real, x.at[pl.ds(0, half)], in_sem.at[0]),
        pltpu.make_async_copy(fake, x.at[pl.ds(half, half)], in_sem.at[1]),
        pltpu.make_async_copy(w1h, w1, in_sem.at[2]),
        pltpu.make_async_copy(w2h, w2, in_sem.at[3]),
    ]
    for c in loads:
        c.start()

    barrier = pltpu.get_barrier_semaphore()
    for j in range(1, nsec):
        pl.semaphore_signal(barrier, inc=1, device_id={"section": sec_at(j)}, device_id_type=MESH)
    for j in range(1, ndp):
        pl.semaphore_signal(barrier, inc=1, device_id={"dp": dp_at(j)}, device_id_type=MESH)

    time = lax.rem(lax.broadcasted_iota(jnp.int32, (rows, width), 0), frames)

    def shift(p, s):
        if s == 0:
            return p
        rolled = pltpu.roll(p, (-s) % rows, 0)
        keep = (time + s >= 0) & (time + s < frames)
        return jnp.where(keep, rolled, 0.0)

    def remote(src, dst, ss, rs, **to):
        c = pltpu.make_async_remote_copy(
            src_ref=src, dst_ref=dst, send_sem=ss, recv_sem=rs, device_id=to, device_id_type=MESH
        )
        c.start()
        return c

    for c in loads[:3]:
        c.wait()
    early = dot(x[:, pl.ds(cin, 2 * cin)], w1[pl.ds(0, 2 * cin), :])
    pre1 = dot(x[...], w1[pl.ds(2 * cin, 3 * cin), :]) + shift(early, -1)
    hall[0] = leaky(pre1)

    pl.semaphore_wait(barrier, nsec - 1 + ndp - 1)
    h_copies = [
        remote(hall.at[0], hall.at[j], hs.at[j - 1], hr.at[j - 1], section=sec_at(j))
        for j in range(1, nsec)
    ]

    def smooth(feature):
        h = feature.astype(F32)
        d = h[:half] - h[half:]
        s = d * d + smooth_width * smooth_width
        inv = lax.rsqrt(s)
        total = jnp.sum(s * inv - smooth_width, axis=0, keepdims=True)
        total = jnp.sum(total, axis=1, keepdims=True)
        q = d * inv * (1.0 / normaliser)
        gate = jnp.where(h > 0, 1.0, leak_slope)
        return total, q, gate

    total1, q1, gate1 = smooth(hall[0])
    slopes[pl.ds(0, half), :] = q1
    slopes[pl.ds(half, half), :] = -q1

    loads[3].wait()
    for j in range(nsec):
        if j:
            h_copies[j - 1].wait_recv()
        owner = lax.rem(sec - j + nsec, nsec)
        block = hall[j]
        part = None
        for k in range(taps):
            p = shift(dot(block, w2[k, pl.ds(pl.multiple_of(owner * width, width), width), :]), k - 2)
            part = p if part is None else part + p
        acc[...] = part if j == 0 else acc[...] + part
    h2 = leaky(acc[...])
    total2, q2, gate2 = smooth(h2)
    line = lax.broadcasted_iota(jnp.int32, lsec.shape[1:], 0)
    lsec[0] = jnp.where(line == 0, total1, jnp.where(line == 1, total2, 0.0))
    l_copies = [
        remote(lsec.at[0], lsec.at[j], lss.at[j - 1], lsr.at[j - 1], section=sec_at(j))
        for j in range(1, nsec)
    ]
    delta2 = jnp.concatenate([q2, -q2], axis=0) * gate2
    for k in range(taps):
        dk[k] = shift(delta2, 2 - k).astype(BF16)

    u_copies = []
    for j in list(range(1, nsec)) + [0]:
        at = pl.multiple_of(sec_at(j) * width, width)
        up = None
        for k in range(taps):
            p = dot(dk[k], w2[k, pl.ds(at, width), :], 1, 1)
            up = p if up is None else up + p
        if j:
            us[j - 1] = up.astype(BF16)
            u_copies.append(
                remote(us.at[j - 1], ur.at[j - 1], uss.at[j - 1], urs.at[j - 1], section=sec_at(j))
            )
        else:
            own_up[...] = up

    for j in range(nsec):
        owner = lax.rem(sec - j + nsec, nsec)
        at = pl.multiple_of(owner * width, width)
        block = hall[j]
        for k in range(taps):
            s2[k, pl.ds(at, width), :] = dot(block, dk[k], 0, 0).astype(BF16)
    g2_copies = []
    for j in range(1, ndp):
        at = pl.multiple_of(dp_at(j) * c2, c2)
        g2_copies.append(
            remote(s2.at[:, pl.ds(at, c2), :], r2.at[j - 1], g2s.at[j - 1], g2r.at[j - 1], dp=dp_at(j))
        )

    up = own_up[...]
    for j in range(1, nsec):
        u_copies[j - 1].wait_recv()
        up = up + ur[j - 1].astype(F32)
    h1 = hall[0].astype(F32)
    delta1 = (slopes[...] + up.astype(BF16).astype(F32)) * jnp.where(h1 > 0, 1.0, leak_slope)
    ahead = shift(delta1, 1).astype(BF16)
    delta1 = delta1.astype(BF16)
    for k in range(taps):
        phase = (k + 1) % 3
        s1[k] = dot(x[:, pl.ds(phase * cin, cin)], ahead if k < 2 else delta1, 0, 0).astype(BF16)
    g1_copies = []
    for j in range(1, ndp):
        at = pl.multiple_of(dp_at(j) * c1, c1)
        g1_copies.append(
            remote(s1.at[:, pl.ds(at, c1), :], r1.at[j - 1], g1s.at[j - 1], g1r.at[j - 1], dp=dp_at(j))
        )

    for c in l_copies:
        c.wait()
    ldp[0] = functools.reduce(
        lambda a, b: a + b, [lsec[lax.rem(sec - g + nsec, nsec)] for g in range(nsec)]
    )
    ld_copies = [
        remote(ldp.at[0], ldp.at[j], lds.at[j - 1], ldr.at[j - 1], dp=dp_at(j)) for j in range(1, ndp)
    ]

    for k in range(taps):
        g2_o[k] = s2[k, pl.ds(pl.multiple_of(dp * c2, c2), c2), :].astype(F32)
        g1_o[k] = s1[k, pl.ds(pl.multiple_of(dp * c1, c1), c1), :].astype(F32)
    for j in range(1, ndp):
        g2_copies[j - 1].wait_recv()
        g2_o[...] += r2[j - 1].astype(F32)
    for j in range(1, ndp):
        g1_copies[j - 1].wait_recv()
        g1_o[...] += r1[j - 1].astype(F32)
    for c in ld_copies:
        c.wait()
    loss_o[...] = functools.reduce(
        lambda a, b: a + b, [ldp[lax.rem(dp - g + ndp, ndp)] for g in range(ndp)]
    )
    for c in h_copies + u_copies + g2_copies + g1_copies:
        c.wait_send()


def shards(ndp, nsec, real_in, fake_in, kernel_first, kernel_second):
    cols, frames_in, cin = real_in.shape
    frames = frames_in // 3
    taps, whole, width = kernel_second.shape
    normaliser = float(cols * frames)
    count_all = float(cols * ndp * frames * whole)
    half = cols * frames
    rows = 2 * half
    c1, c2 = cin // ndp, whole // ndp
    dma = pltpu.SemaphoreType.DMA
    loss, g1, g2 = pl.pallas_call(
        functools.partial(kernel, ndp, nsec, frames, normaliser),
        out_shape=(
            jax.ShapeDtypeStruct((8, 128), F32),
            jax.ShapeDtypeStruct((taps, c1, width), F32),
            jax.ShapeDtypeStruct((taps, c2, width), F32),
        ),
        in_specs=[pl.BlockSpec(memory_space=pl.ANY)] * 4,
        out_specs=(pl.BlockSpec(memory_space=pltpu.VMEM),) * 3,
        scratch_shapes=[
            pltpu.VMEM((rows, 3 * cin), BF16),
            pltpu.VMEM((taps * cin, width), BF16),
            pltpu.VMEM((taps, whole, width), BF16),
            pltpu.VMEM((nsec, rows, width), BF16),
            pltpu.VMEM((rows, width), F32),
            pltpu.VMEM((rows, width), F32),
            pltpu.VMEM((taps, rows, width), BF16),
            pltpu.VMEM((nsec - 1, rows, width), BF16),
            pltpu.VMEM((nsec - 1, rows, width), BF16),
            pltpu.VMEM((rows, width), F32),
            pltpu.VMEM((taps, whole, width), BF16),
            pltpu.VMEM((taps, cin, width), BF16),
            pltpu.VMEM((ndp - 1, taps, c2, width), BF16),
            pltpu.VMEM((ndp - 1, taps, c1, width), BF16),
            pltpu.VMEM((nsec, 8, 128), F32),
            pltpu.VMEM((ndp, 8, 128), F32),
            dma((4,)),
            dma((nsec - 1,)), dma((nsec - 1,)),
            dma((nsec - 1,)), dma((nsec - 1,)),
            dma((ndp - 1,)), dma((ndp - 1,)),
            dma((ndp - 1,)), dma((ndp - 1,)),
            dma((nsec - 1,)), dma((nsec - 1,)),
            dma((ndp - 1,)), dma((ndp - 1,)),
        ],
        compiler_params=pltpu.CompilerParams(collective_id=0, has_side_effects=True),
    )(
        real_in.reshape(half, 3 * cin),
        fake_in.reshape(half, 3 * cin),
        kernel_first.reshape(taps * cin, width),
        kernel_second,
    )
    return loss[:2, 0] / count_all, g1.transpose(1, 0, 2), g2.transpose(1, 0, 2)


def solution(mesh):
    return jax.shard_map(
        functools.partial(shards, mesh.shape["dp"], mesh.shape["section"]),
        mesh=mesh,
        in_specs=(
            P("dp", None, None),
            P("dp", None, None),
            P(None, None, "section"),
            P(None, None, "section"),
        ),
        out_specs=(P(), P("dp", None, "section"), P("dp", None, "section")),
        check_vma=False,
    )
```

time: 298 us -> 127 us (0.43)
  waiting for transfers between devices: 181 us -> 0 us
  Pallas kernels: 0 us -> 116 us
  blocking collectives: 42.5 us -> 0 us
  matrix products: 26.1 us -> 0 us
  local copies, waits for them, and re-layouts: 24.7 us -> 8.22 us
  between operations: 14 us -> 0.65 us
  other arithmetic: 8.82 us -> 1.31 us
    reduce_scatter x3 -> x0, waiting for transfers between devices: 159 us -> none  [the longest x1 75.2 us: shards(): lax.psum_scatter(term_first, 'dp', scatter_dimension=0, tiled=True)]
    pallas_call x0 -> x1, Pallas kernels: none -> 116 us  [shards(): pl.pallas_call(functools.partial(kernel, ndp, nsec, frames, normaliser),...]
    psum x1 -> x0, blocking collectives: 42.5 us -> none  [shards(): total_second = lax.psum(partial_second, ('dp', 'section'))]
    dot_general x25 -> x0, matrix products: 26.1 us -> none  [the longest x10 14.1 us: weight_term(): lax.dot_general(window, flat_delta, (((0,), (0,)), ((), ())), preferred_e...]
    all_gather x1 -> x0, waiting for transfers between devices: 22.6 us -> none  [shards(): whole_first = lax.all_gather(first, 'section', axis=2, tiled=True)]
    slice x7 -> x0, local copies, waits for them, and re-layouts: 21.4 us -> none  [the longest x5 14.6 us: conv_strided(): window = padded[:, tap:tap + 3 * frames - 2:3].reshape(-1, values.shape[2])]
    reshape x0 -> x2, local copies, waits for them, and re-layouts: none -> 4.5 us  [the longest x1 3.11 us: shards(): real_in.reshape(half, 3 * cin)]
  transfers between devices with their start and end apart: 4 -> 0, of which waited for: 4 -> 0; matrix products, arithmetic and copies ran while one was open for 6% -> 0% of each run, Pallas kernels for 0% -> 0%
where the time goes in v1:
time: 127 us; the launch traced here: 126 us
  Pallas kernels  116 us (91%)
  local copies, waits for them, and re-layouts  8.22 us (6%)
  other arithmetic  1.31 us (1%)
    pallas_call x1, Pallas kernels, shards(): pl.pallas_call(functools.partial(kernel, ndp, nsec, frames, normaliser),...  116 us
    unnamed x4, local copies, waits for them, and re-layouts  3.72 us
    reshape x1, local copies, waits for them, and re-layouts, shards(): real_in.reshape(half, 3 * cin)  3.11 us

profile of v1, /device:TPU:0, one launch (start us, length us, event | category | flops | bytes accessed | tf_op | source)
XLA Modules:
  0.0 126.1 jit_solution(12896369795549684883)
XLA Ops:
  0.6 0.0 copy-start
  0.6 3.1 %reshape.17.real = bf16[384,1536]{1,0:T(8,128)(2,1)} reshape(bf16[8,144,512]{2,1,0:T(8,128)(2,1)} %param.4) | data formatting | bytes 2359296 | tf_op jit(solution)/shard_map/reshape | solution.py:245
  3.8 0.0 copy-done
  3.8 1.4 %reshape.18.fake = bf16[384,1536]{1,0:T(8,128)(2,1)} reshape(bf16[8,144,512]{2,1,0:T(8,128)(2,1)S(1)} %copy-done) | data formatting | bytes 2359296 | tf_op jit(solution)/shard_map/reshape | solution.py:246
  5.1 116.0 %shard_map.67 = (f32[8,128]{1,0:T(8,128)}, f32[5,64,256]{2,1,0:T(8,128)}, f32[5,128,256]{2,1,0:T(8,128)}) custom-call(bf16[384,1536]{1,0:T(8,128)(2,1)} %reshape.17.real, bf16[384,1536]{1,0:T(8,128)(2,1)} %reshape.18.fake, bf16[2560,256]{1,0:T(8,128)(2,1)} %bitcast.3, bf16[5,1024,256]{2,1,0:T(8,128)(2,1)} %w2h.1), custom_call_target="tpu_custom_call" | custom-call | tf_op jit(solution)/shard_map/pallas_call | solution.py:209
  121.1 1.3 %multiply_reduce_fusion = f32[2]{0:T(128)} fusion(f32[8,128]{1,0:T(8,128)} %get-tuple-element.6), kind=kLoop, calls=%fused_computation | loop fusion | flops 2 | bytes 16 | tf_op jit(solution)/shard_map/div | solution.py:250
  122.4 1.7 %copy.9 = f32[64,5,256]{2,0,1:T(8,128)} copy(f32[64,5,256]{2,0,1:T(8,128)} %bitcast.5) | data formatting | bytes 655360
  124.1 2.0 %copy.10 = f32[128,5,256]{2,0,1:T(8,128)} copy(f32[128,5,256]{2,0,1:T(8,128)} %bitcast.4) | data formatting | bytes 1310720
Async XLA Ops:
  0.6 3.1 %copy-start = (bf16[8,144,512]{2,1,0:T(8,128)(2,1)S(1)}, bf16[8,144,512]{2,1,0:T(8,128)(2,1)}, u32[]{:S(2)}) copy-start(bf16[8,144,512]{2,1,0:T(8,128)(2,1)} %param.5) | copy-start | bytes 3538948

commit v2 on v1

--- a/solution.py
+++ b/solution.py
@@ -26,8 +26,8 @@
     ndp, nsec, frames, normaliser,
     real, fake, w1h, w2h,
     loss_o, g1_o, g2_o,
-    x, w1, w2, hall, acc, slopes, dk, us, ur, own_up, s2, s1, r2, r1, lsec, ldp,
-    in_sem, hs, hr, uss, urs, g2s, g2r, g1s, g1r, lss, lsr, lds, ldr,
+    x, w1, w2, hall, acc, slopes, dk, us, ur, own_up, s2, s1, y2, y1, z2, z1, r2, r1, lsec, ldp,
+    in_sem, hs, hr, uss, urs, y2s, y2r, y1s, y1r, z2s, z2r, z1s, z1r, lss, lsr, lds, ldr,
 ):
     dp, sec = lax.axis_index("dp"), lax.axis_index("section")
     rows, width = acc.shape
@@ -35,6 +35,22 @@
     taps = w2.shape[0]
     cin = g1_o.shape[1] * ndp
     c2, c1 = g2_o.shape[1], g1_o.shape[1]
+
+    inner, outer = lax.rem(dp, 2), dp // 2
+    nout = ndp // 2
+    span = nout // nsec
+    group, place = outer // span, lax.rem(outer, span)
+    partner = dp + 1 - 2 * inner
+    sec_inner, sec_outer = lax.rem(sec, 2), sec // 2
+    sec_outers = nsec // 2
+    sec_partner = sec + 1 - 2 * sec_inner
+
+    def owner_of(slot):
+        jo, ji = slot // 2, slot % 2
+        return lax.rem(sec_outer - jo + sec_outers, sec_outers) * 2 + lax.rem(sec_inner + ji, 2)
+
+    def outer_at(jb, i):
+        return lax.rem(group + jb, nsec) * span + lax.rem(place + i, span)
 
     def sec_at(j):
         return lax.rem(sec + j, nsec)
@@ -80,10 +96,18 @@
     hall[0] = leaky(pre1)
 
     pl.semaphore_wait(barrier, nsec - 1 + ndp - 1)
-    h_copies = [
-        remote(hall.at[0], hall.at[j], hs.at[j - 1], hr.at[j - 1], section=sec_at(j))
-        for j in range(1, nsec)
-    ]
+    halves = [pl.ds(0, half), pl.ds(half, half)]
+    h_direct, h_passed = {}, {}
+    for c, at in enumerate(halves):
+        for jo in range(1, sec_outers):
+            to = lax.rem(sec_outer + jo, sec_outers) * 2 + sec_inner
+            h_direct[2 * jo, c] = remote(
+                hall.at[0, at], hall.at[2 * jo, at], hs.at[2 * jo, c], hr.at[2 * jo, c], section=to
+            )
+    for c, at in enumerate(halves):
+        h_direct[1, c] = remote(
+            hall.at[0, at], hall.at[1, at], hs.at[1, c], hr.at[1, c], section=sec_partner
+        )
 
     def smooth(feature):
         h = feature.astype(F32)
@@ -102,9 +126,21 @@
 
     loads[3].wait()
     for j in range(nsec):
-        if j:
-            h_copies[j - 1].wait_recv()
-        owner = lax.rem(sec - j + nsec, nsec)
+        if j == 2:
+            for c, at in enumerate(halves):
+                for jo in range(1, sec_outers):
+                    h_direct[2 * jo, c].wait_recv()
+                    h_passed[2 * jo + 1, c] = remote(
+                        hall.at[2 * jo, at],
+                        hall.at[2 * jo + 1, at],
+                        hs.at[2 * jo + 1, c],
+                        hr.at[2 * jo + 1, c],
+                        section=sec_partner,
+                    )
+        if j % 2:
+            for c in range(2):
+                (h_direct if j == 1 else h_passed)[j, c].wait_recv()
+        owner = owner_of(j)
         block = hall[j]
         part = None
         for k in range(taps):
@@ -123,6 +159,43 @@
     for k in range(taps):
         dk[k] = shift(delta2, 2 - k).astype(BF16)
 
+    order = [(jb, i) for jb in range(1, nsec) for i in range(span)] + [(0, i) for i in range(1, span)] + [(0, 0)]
+
+    def exchange(send, land, ss, rs, rows_of, group_at):
+        copies = []
+        for n, (jb, i) in enumerate(order):
+            if jb != group_at:
+                continue
+            at = pl.multiple_of((outer_at(jb, i) * 2 + 1 - inner) * rows_of, rows_of)
+            copies.append(
+                remote(send.at[:, pl.ds(at, rows_of), :], land.at[n], ss.at[n], rs.at[n], dp=partner)
+            )
+        return copies
+
+    def relay(copy, n, send, land, out, pair, final, ss, rs, rows_of):
+        jb, i = order[n]
+        to = outer_at(jb, i)
+        at = pl.multiple_of((to * 2 + inner) * rows_of, rows_of)
+        copy.wait_recv()
+        both = send[:, pl.ds(at, rows_of), :].astype(F32) + land[n].astype(F32)
+        if n == nout - 1:
+            out[...] = both
+            return None
+        pair[n] = both.astype(BF16)
+        return remote(pair.at[n], final.at[n], ss.at[n], rs.at[n], dp=to * 2 + inner)
+
+    y2c, z2c, y1c, z1c = [], [], [], []
+    for jb in list(range(1, nsec)) + [0]:
+        owner = lax.rem(group + jb, nsec)
+        slot = lax.rem(sec_outer - owner // 2 + sec_outers, sec_outers) * 2 + lax.rem(
+            sec_inner + lax.rem(owner, 2), 2
+        )
+        at = pl.multiple_of(owner * width, width)
+        block = hall[slot]
+        for k in range(taps):
+            s2[k, pl.ds(at, width), :] = dot(block, dk[k], 0, 0).astype(BF16)
+        y2c += exchange(s2, y2, y2s, y2r, c2, jb)
+
     u_copies = []
     for j in list(range(1, nsec)) + [0]:
         at = pl.multiple_of(sec_at(j) * width, width)
@@ -138,18 +211,17 @@
         else:
             own_up[...] = up
 
-    for j in range(nsec):
-        owner = lax.rem(sec - j + nsec, nsec)
-        at = pl.multiple_of(owner * width, width)
-        block = hall[j]
-        for k in range(taps):
-            s2[k, pl.ds(at, width), :] = dot(block, dk[k], 0, 0).astype(BF16)
-    g2_copies = []
-    for j in range(1, ndp):
-        at = pl.multiple_of(dp_at(j) * c2, c2)
-        g2_copies.append(
-            remote(s2.at[:, pl.ds(at, c2), :], r2.at[j - 1], g2s.at[j - 1], g2r.at[j - 1], dp=dp_at(j))
-        )
+    for c in l_copies:
+        c.wait()
+    ldp[0] = functools.reduce(
+        lambda a, b: a + b, [lsec[lax.rem(sec - g + nsec, nsec)] for g in range(nsec)]
+    )
+    ld_copies = [
+        remote(ldp.at[0], ldp.at[j], lds.at[j - 1], ldr.at[j - 1], dp=dp_at(j)) for j in range(1, ndp)
+    ]
+
+    for n in range(nout - 1):
+        z2c.append(relay(y2c[n], n, s2, y2, g2_o, z2, r2, z2s, z2r, c2))
 
     up = own_up[...]
     for j in range(1, nsec):
@@ -162,37 +234,25 @@
     for k in range(taps):
         phase = (k + 1) % 3
         s1[k] = dot(x[:, pl.ds(phase * cin, cin)], ahead if k < 2 else delta1, 0, 0).astype(BF16)
-    g1_copies = []
-    for j in range(1, ndp):
-        at = pl.multiple_of(dp_at(j) * c1, c1)
-        g1_copies.append(
-            remote(s1.at[:, pl.ds(at, c1), :], r1.at[j - 1], g1s.at[j - 1], g1r.at[j - 1], dp=dp_at(j))
-        )
-
-    for c in l_copies:
-        c.wait()
-    ldp[0] = functools.reduce(
-        lambda a, b: a + b, [lsec[lax.rem(sec - g + nsec, nsec)] for g in range(nsec)]
-    )
-    ld_copies = [
-        remote(ldp.at[0], ldp.at[j], lds.at[j - 1], ldr.at[j - 1], dp=dp_at(j)) for j in range(1, ndp)
-    ]
-
-    for k in range(taps):
-        g2_o[k] = s2[k, pl.ds(pl.multiple_of(dp * c2, c2), c2), :].astype(F32)
-        g1_o[k] = s1[k, pl.ds(pl.multiple_of(dp * c1, c1), c1), :].astype(F32)
-    for j in range(1, ndp):
-        g2_copies[j - 1].wait_recv()
-        g2_o[...] += r2[j - 1].astype(F32)
-    for j in range(1, ndp):
-        g1_copies[j - 1].wait_recv()
-        g1_o[...] += r1[j - 1].astype(F32)
+    for jb in list(range(1, nsec)) + [0]:
+        y1c += exchange(s1, y1, y1s, y1r, c1, jb)
+
+    relay(y2c[-1], nout - 1, s2, y2, g2_o, z2, r2, z2s, z2r, c2)
+    for n in range(nout - 1):
+        z2c[n].wait_recv()
+        g2_o[...] += r2[n].astype(F32)
+    for n in range(nout):
+        z1c.append(relay(y1c[n], n, s1, y1, g1_o, z1, r1, z1s, z1r, c1))
+    z1c = z1c[:-1]
     for c in ld_copies:
         c.wait()
     loss_o[...] = functools.reduce(
         lambda a, b: a + b, [ldp[lax.rem(dp - g + ndp, ndp)] for g in range(ndp)]
     )
-    for c in h_copies + u_copies + g2_copies + g1_copies:
+    for n in range(nout - 1):
+        z1c[n].wait_recv()
+        g1_o[...] += r1[n].astype(F32)
+    for c in list(h_direct.values()) + list(h_passed.values()) + u_copies + y2c + z2c + y1c + z1c:
         c.wait_send()
 
 
@@ -205,6 +265,7 @@
     half = cols * frames
     rows = 2 * half
     c1, c2 = cin // ndp, whole // ndp
+    nout = ndp // 2
     dma = pltpu.SemaphoreType.DMA
     loss, g1, g2 = pl.pallas_call(
         functools.partial(kernel, ndp, nsec, frames, normaliser),
@@ -228,15 +289,19 @@
             pltpu.VMEM((rows, width), F32),
             pltpu.VMEM((taps, whole, width), BF16),
             pltpu.VMEM((taps, cin, width), BF16),
-            pltpu.VMEM((ndp - 1, taps, c2, width), BF16),
-            pltpu.VMEM((ndp - 1, taps, c1, width), BF16),
+            pltpu.VMEM((nout, taps, c2, width), BF16),
+            pltpu.VMEM((nout, taps, c1, width), BF16),
+            pltpu.VMEM((nout, taps, c2, width), BF16),
+            pltpu.VMEM((nout, taps, c1, width), BF16),
+            pltpu.VMEM((nout, taps, c2, width), BF16),
+            pltpu.VMEM((nout, taps, c1, width), BF16),
             pltpu.VMEM((nsec, 8, 128), F32),
             pltpu.VMEM((ndp, 8, 128), F32),
             dma((4,)),
+            dma((nsec, 2)), dma((nsec, 2)),
             dma((nsec - 1,)), dma((nsec - 1,)),
-            dma((nsec - 1,)), dma((nsec - 1,)),
-            dma((ndp - 1,)), dma((ndp - 1,)),
-            dma((ndp - 1,)), dma((ndp - 1,)),
+            dma((nout,)), dma((nout,)), dma((nout,)), dma((nout,)),
+            dma((nout,)), dma((nout,)), dma((nout,)), dma((nout,)),
             dma((nsec - 1,)), dma((nsec - 1,)),
             dma((ndp - 1,)), dma((ndp - 1,)),
         ],

time: 127 us -> 86.8 us (0.68)
  the two profiles are of different devices: /device:TPU:0 before, /device:TPU:24 now
where the time goes in v2:
time: 86.8 us; the launch traced here: 86.5 us
  Pallas kernels  76.3 us (88%)
  local copies, waits for them, and re-layouts  8.22 us (9%)
  other arithmetic  1.31 us (2%)
    pallas_call x1, Pallas kernels, shards(): pl.pallas_call(functools.partial(kernel, ndp, nsec, frames, normaliser),...  76.3 us
    unnamed x4, local copies, waits for them, and re-layouts  3.72 us
    reshape x1, local copies, waits for them, and re-layouts, shards(): real_in.reshape(half, 3 * cin)  3.11 us

profile of v2, /device:TPU:24, one launch (start us, length us, event | category | flops | bytes accessed | tf_op | source)
XLA Modules:
  0.0 86.5 jit_solution(16178425968731982250)
XLA Ops:
  0.6 0.0 copy-start
  0.6 3.1 %reshape.17.real = bf16[384,1536]{1,0:T(8,128)(2,1)} reshape(bf16[8,144,512]{2,1,0:T(8,128)(2,1)} %param.4) | data formatting | bytes 2359296 | tf_op jit(solution)/shard_map/reshape | solution.py:310
  3.8 0.0 copy-done
  3.8 1.4 %reshape.18.fake = bf16[384,1536]{1,0:T(8,128)(2,1)} reshape(bf16[8,144,512]{2,1,0:T(8,128)(2,1)S(1)} %copy-done) | data formatting | bytes 2359296 | tf_op jit(solution)/shard_map/reshape | solution.py:311
  5.1 76.3 %shard_map.67 = (f32[8,128]{1,0:T(8,128)}, f32[5,64,256]{2,1,0:T(8,128)}, f32[5,128,256]{2,1,0:T(8,128)}) custom-call(bf16[384,1536]{1,0:T(8,128)(2,1)} %reshape.17.real, bf16[384,1536]{1,0:T(8,128)(2,1)} %reshape.18.fake, bf16[2560,256]{1,0:T(8,128)(2,1)} %bitcast.3, bf16[5,1024,256]{2,1,0:T(8,128)(2,1)} %w2h.1), custom_call_target="tpu_custom_call" | custom-call | tf_op jit(solution)/shard_map/pallas_call | solution.py:270
  81.5 1.3 %multiply_reduce_fusion = f32[2]{0:T(128)} fusion(f32[8,128]{1,0:T(8,128)} %get-tuple-element.6), kind=kLoop, calls=%fused_computation | loop fusion | flops 2 | bytes 16 | tf_op jit(solution)/shard_map/div | solution.py:315
  82.8 1.7 %copy.9 = f32[64,5,256]{2,0,1:T(8,128)} copy(f32[64,5,256]{2,0,1:T(8,128)} %bitcast.5) | data formatting | bytes 655360
  84.5 2.0 %copy.10 = f32[128,5,256]{2,0,1:T(8,128)} copy(f32[128,5,256]{2,0,1:T(8,128)} %bitcast.4) | data formatting | bytes 1310720
Async XLA Ops:
  0.6 3.1 %copy-start = (bf16[8,144,512]{2,1,0:T(8,128)(2,1)S(1)}, bf16[8,144,512]{2,1,0:T(8,128)(2,1)}, u32[]{:S(2)}) copy-start(bf16[8,144,512]{2,1,0:T(8,128)(2,1)} %param.5) | copy-start | bytes 3538948

commit v3 on v2

--- a/solution.py
+++ b/solution.py
@@ -26,7 +26,7 @@
     ndp, nsec, frames, normaliser,
     real, fake, w1h, w2h,
     loss_o, g1_o, g2_o,
-    x, w1, w2, hall, acc, slopes, dk, us, ur, own_up, s2, s1, y2, y1, z2, z1, r2, r1, lsec, ldp,
+    raw, wide, x, w1, w2, hall, acc, slopes, dk, us, ur, own_up, s2, s1, y2, y1, z2, z1, r2, r1, lsec, ldp,
     in_sem, hs, hr, uss, urs, y2s, y2r, y1s, y1r, z2s, z2r, z1s, z1r, lss, lsr, lds, ldr,
 ):
     dp, sec = lax.axis_index("dp"), lax.axis_index("section")
@@ -59,9 +59,9 @@
         return lax.rem(dp + j, ndp)
 
     loads = [
-        pltpu.make_async_copy(real, x.at[pl.ds(0, half)], in_sem.at[0]),
-        pltpu.make_async_copy(fake, x.at[pl.ds(half, half)], in_sem.at[1]),
+        pltpu.make_async_copy(real, raw.at[0], in_sem.at[0]),
         pltpu.make_async_copy(w1h, w1, in_sem.at[2]),
+        pltpu.make_async_copy(fake, raw.at[1], in_sem.at[1]),
         pltpu.make_async_copy(w2h, w2, in_sem.at[3]),
     ]
     for c in loads:
@@ -78,8 +78,9 @@
     def shift(p, s):
         if s == 0:
             return p
-        rolled = pltpu.roll(p, (-s) % rows, 0)
-        keep = (time + s >= 0) & (time + s < frames)
+        rolled = pltpu.roll(p, (-s) % p.shape[0], 0)
+        at = time[: p.shape[0]]
+        keep = (at + s >= 0) & (at + s < frames)
         return jnp.where(keep, rolled, 0.0)
 
     def remote(src, dst, ss, rs, **to):
@@ -89,22 +90,27 @@
         c.start()
         return c
 
-    for c in loads[:3]:
-        c.wait()
-    early = dot(x[:, pl.ds(cin, 2 * cin)], w1[pl.ds(0, 2 * cin), :])
-    pre1 = dot(x[...], w1[pl.ds(2 * cin, 3 * cin), :]) + shift(early, -1)
-    hall[0] = leaky(pre1)
-
-    pl.semaphore_wait(barrier, nsec - 1 + ndp - 1)
     halves = [pl.ds(0, half), pl.ds(half, half)]
     h_direct, h_passed = {}, {}
     for c, at in enumerate(halves):
+        loads[2 * c].wait()
+        for b in range(cin // 128):
+            wide[c * (cin // 128) + b] = raw[c, :, pl.ds(b * 128, 128)].astype(F32)
+            for phase in range(3):
+                lanes = wide[c * (cin // 128) + b, pl.ds(phase, half, stride=3), :]
+                x[at, pl.ds(phase * cin + b * 128, 128)] = lanes.astype(BF16)
+        if c == 0:
+            loads[1].wait()
+        early = dot(x[at, pl.ds(cin, 2 * cin)], w1[pl.ds(0, 2 * cin), :])
+        pre1 = dot(x[at, :], w1[pl.ds(2 * cin, 3 * cin), :]) + shift(early, -1)
+        hall[0, at] = leaky(pre1)
+        if c == 0:
+            pl.semaphore_wait(barrier, nsec - 1 + ndp - 1)
         for jo in range(1, sec_outers):
             to = lax.rem(sec_outer + jo, sec_outers) * 2 + sec_inner
             h_direct[2 * jo, c] = remote(
                 hall.at[0, at], hall.at[2 * jo, at], hs.at[2 * jo, c], hr.at[2 * jo, c], section=to
             )
-    for c, at in enumerate(halves):
         h_direct[1, c] = remote(
             hall.at[0, at], hall.at[1, at], hs.at[1, c], hr.at[1, c], section=sec_partner
         )
@@ -161,30 +167,50 @@
 
     order = [(jb, i) for jb in range(1, nsec) for i in range(span)] + [(0, i) for i in range(1, span)] + [(0, 0)]
 
-    def exchange(send, land, ss, rs, rows_of, group_at):
-        copies = []
+    pieces = [pl.ds(0, taps // 2), pl.ds(taps // 2, taps - taps // 2)]
+
+    def exchange(copies, send, land, ss, rs, rows_of, group_at, piece):
+        cut = pieces[piece]
         for n, (jb, i) in enumerate(order):
             if jb != group_at:
                 continue
             at = pl.multiple_of((outer_at(jb, i) * 2 + 1 - inner) * rows_of, rows_of)
-            copies.append(
-                remote(send.at[:, pl.ds(at, rows_of), :], land.at[n], ss.at[n], rs.at[n], dp=partner)
+            copies[n, piece] = remote(
+                send.at[cut, pl.ds(at, rows_of), :],
+                land.at[n, cut],
+                ss.at[n, piece],
+                rs.at[n, piece],
+                dp=partner,
             )
-        return copies
-
-    def relay(copy, n, send, land, out, pair, final, ss, rs, rows_of):
+
+    def relay(copies, n, piece, send, land, out, pair, final, ss, rs, rows_of):
+        cut = pieces[piece]
         jb, i = order[n]
         to = outer_at(jb, i)
         at = pl.multiple_of((to * 2 + inner) * rows_of, rows_of)
-        copy.wait_recv()
-        both = send[:, pl.ds(at, rows_of), :].astype(F32) + land[n].astype(F32)
+        copies[n, piece].wait_recv()
+        both = send[cut, pl.ds(at, rows_of), :].astype(F32) + land[n, cut].astype(F32)
         if n == nout - 1:
-            out[...] = both
-            return None
-        pair[n] = both.astype(BF16)
-        return remote(pair.at[n], final.at[n], ss.at[n], rs.at[n], dp=to * 2 + inner)
-
-    y2c, z2c, y1c, z1c = [], [], [], []
+            out[cut] = both
+            return []
+        pair[n, cut] = both.astype(BF16)
+        return [
+            remote(
+                pair.at[n, cut],
+                final.at[n, cut],
+                ss.at[n, piece],
+                rs.at[n, piece],
+                dp=to * 2 + inner,
+            )
+        ]
+
+    def relay2(n, piece):
+        return relay(y2c, n, piece, s2, y2, g2_o, z2, r2, z2s, z2r, c2)
+
+    def relay1(n, piece):
+        return relay(y1c, n, piece, s1, y1, g1_o, z1, r1, z1s, z1r, c1)
+
+    y2c, z2c, y1c, z1c = {}, [], {}, []
     for jb in list(range(1, nsec)) + [0]:
         owner = lax.rem(group + jb, nsec)
         slot = lax.rem(sec_outer - owner // 2 + sec_outers, sec_outers) * 2 + lax.rem(
@@ -192,9 +218,10 @@
         )
         at = pl.multiple_of(owner * width, width)
         block = hall[slot]
-        for k in range(taps):
-            s2[k, pl.ds(at, width), :] = dot(block, dk[k], 0, 0).astype(BF16)
-        y2c += exchange(s2, y2, y2s, y2r, c2, jb)
+        for piece, cut in enumerate(pieces):
+            for k in range(cut.start, cut.start + cut.size):
+                s2[k, pl.ds(at, width), :] = dot(block, dk[k], 0, 0).astype(BF16)
+            exchange(y2c, s2, y2, y2s, y2r, c2, jb, piece)
 
     u_copies = []
     for j in list(range(1, nsec)) + [0]:
@@ -221,7 +248,7 @@
     ]
 
     for n in range(nout - 1):
-        z2c.append(relay(y2c[n], n, s2, y2, g2_o, z2, r2, z2s, z2r, c2))
+        z2c += relay2(n, 0) + relay2(n, 1)
 
     up = own_up[...]
     for j in range(1, nsec):
@@ -231,28 +258,34 @@
     delta1 = (slopes[...] + up.astype(BF16).astype(F32)) * jnp.where(h1 > 0, 1.0, leak_slope)
     ahead = shift(delta1, 1).astype(BF16)
     delta1 = delta1.astype(BF16)
-    for k in range(taps):
-        phase = (k + 1) % 3
-        s1[k] = dot(x[:, pl.ds(phase * cin, cin)], ahead if k < 2 else delta1, 0, 0).astype(BF16)
+    for piece, cut in enumerate(pieces):
+        for k in range(cut.start, cut.start + cut.size):
+            phase = (k + 1) % 3
+            s1[k] = dot(x[:, pl.ds(phase * cin, cin)], ahead if k < 2 else delta1, 0, 0).astype(BF16)
     for jb in list(range(1, nsec)) + [0]:
-        y1c += exchange(s1, y1, y1s, y1r, c1, jb)
-
-    relay(y2c[-1], nout - 1, s2, y2, g2_o, z2, r2, z2s, z2r, c2)
+        for piece in range(2):
+            exchange(y1c, s1, y1, y1s, y1r, c1, jb, piece)
+
+    relay2(nout - 1, 0)
+    relay2(nout - 1, 1)
     for n in range(nout - 1):
-        z2c[n].wait_recv()
+        z1c += relay1(n, 0) + relay1(n, 1)
+        z2c[2 * n].wait_recv()
+        z2c[2 * n + 1].wait_recv()
         g2_o[...] += r2[n].astype(F32)
-    for n in range(nout):
-        z1c.append(relay(y1c[n], n, s1, y1, g1_o, z1, r1, z1s, z1r, c1))
-    z1c = z1c[:-1]
+    relay1(nout - 1, 0)
+    relay1(nout - 1, 1)
     for c in ld_copies:
         c.wait()
     loss_o[...] = functools.reduce(
         lambda a, b: a + b, [ldp[lax.rem(dp - g + ndp, ndp)] for g in range(ndp)]
     )
     for n in range(nout - 1):
-        z1c[n].wait_recv()
+        z1c[2 * n].wait_recv()
+        z1c[2 * n + 1].wait_recv()
         g1_o[...] += r1[n].astype(F32)
-    for c in list(h_direct.values()) + list(h_passed.values()) + u_copies + y2c + z2c + y1c + z1c:
+    started = list(h_direct.values()) + list(h_passed.values()) + list(y2c.values())
+    for c in started + list(y1c.values()) + u_copies + z2c + z1c:
         c.wait_send()
 
 
@@ -277,6 +310,8 @@
         in_specs=[pl.BlockSpec(memory_space=pl.ANY)] * 4,
         out_specs=(pl.BlockSpec(memory_space=pltpu.VMEM),) * 3,
         scratch_shapes=[
+            pltpu.VMEM((2, 3 * half, cin), BF16),
+            pltpu.VMEM((2 * cin // 128, 3 * half, 128), F32),
             pltpu.VMEM((rows, 3 * cin), BF16),
             pltpu.VMEM((taps * cin, width), BF16),
             pltpu.VMEM((taps, whole, width), BF16),
@@ -300,15 +335,15 @@
             dma((4,)),
             dma((nsec, 2)), dma((nsec, 2)),
             dma((nsec - 1,)), dma((nsec - 1,)),
-            dma((nout,)), dma((nout,)), dma((nout,)), dma((nout,)),
-            dma((nout,)), dma((nout,)), dma((nout,)), dma((nout,)),
+            dma((nout, 2)), dma((nout, 2)), dma((nout, 2)), dma((nout, 2)),
+            dma((nout, 2)), dma((nout, 2)), dma((nout, 2)), dma((nout, 2)),
             dma((nsec - 1,)), dma((nsec - 1,)),
             dma((ndp - 1,)), dma((ndp - 1,)),
         ],
         compiler_params=pltpu.CompilerParams(collective_id=0, has_side_effects=True),
     )(
-        real_in.reshape(half, 3 * cin),
-        fake_in.reshape(half, 3 * cin),
+        real_in.reshape(3 * half, cin),
+        fake_in.reshape(3 * half, cin),
         kernel_first.reshape(taps * cin, width),
         kernel_second,
     )

time: 86.8 us -> 78.4 us (0.903)
  the two profiles are of different devices: /device:TPU:24 before, /device:TPU:0 now
where the time goes in v3:
time: 78.4 us; the launch traced here: 77 us
  Pallas kernels  71.4 us (91%)
  local copies, waits for them, and re-layouts  3.71 us (5%)
  other arithmetic  1.3 us (2%)
    pallas_call x1, Pallas kernels, shards(): pl.pallas_call(functools.partial(kernel, ndp, nsec, frames, normaliser),...  71.4 us
    unnamed x2, local copies, waits for them, and re-layouts  3.71 us

profile of v3, /device:TPU:0, one launch (start us, length us, event | category | flops | bytes accessed | tf_op | source)
XLA Modules:
  0.0 77.0 jit_solution(12010203867963496874)
XLA Ops:
  0.6 71.4 %shard_map.67 = (f32[8,128]{1,0:T(8,128)}, f32[5,64,256]{2,1,0:T(8,128)}, f32[5,128,256]{2,1,0:T(8,128)}) custom-call(bf16[1152,512]{1,0:T(8,128)(2,1)} %bitcast.6, bf16[1152,512]{1,0:T(8,128)(2,1)} %bitcast.7, bf16[2560,256]{1,0:T(8,128)(2,1)} %bitcast.5, bf16[5,1024,256]{2,1,0:T(8,128)(2,1)} %w2h.1), custom_call_target="tpu_custom_call" | custom-call | tf_op jit(solution)/shard_map/pallas_call | solution.py:303
  72.0 1.3 %multiply_reduce_fusion = f32[2]{0:T(128)} fusion(f32[8,128]{1,0:T(8,128)} %get-tuple-element.6), kind=kLoop, calls=%fused_computation | loop fusion | flops 2 | bytes 16 | tf_op jit(solution)/shard_map/div | solution.py:350
  73.3 1.7 %copy.9 = f32[64,5,256]{2,0,1:T(8,128)} copy(f32[64,5,256]{2,0,1:T(8,128)} %bitcast.9) | data formatting | bytes 655360
  75.0 2.0 %copy.10 = f32[128,5,256]{2,0,1:T(8,128)} copy(f32[128,5,256]{2,0,1:T(8,128)} %bitcast.8) | data formatting | bytes 1310720
